TPU v7x, 32 devices: a whole 2x2x4 slice. The times are simulated.
32 devices in a mesh: dp: 4 (over x, core), rows: 8 (over z, y).
Axes of the slice: x: 2, y: 2, z: 4, core: 2. Of those that a mesh axis runs over, the one named last changes fastest.
Arguments:
- item_table: float32 [131072, 128], P(('dp', 'rows')), may hold values from -3 to 3
- adagrad_state: float32 [131072, 128], P(('dp', 'rows')), may hold values from 0.0001 to 0.01
- history_ids: int32 [4096, 50], P(('dp', 'rows')), may hold values from 0 to 131071, as said below
- positive_ids: int32 [4096], P(('dp', 'rows')), may hold values from 0 to 131071, as said below
Outputs:
- new_table: float32 [131072, 128], P(('dp', 'rows'))
- new_state: float32 [131072, 128], P(('dp', 'rows'))
Inputs may be any that keep to these rules, and one draw needn't show every extreme that they name: `history_ids`: ids are counted over one device's 128 users (an aligned block of users), history and positive together, with repeats. In every such block, at most 512 ids have any one value of id // 4096, and some value has exactly 512; one value has exactly 512 in every block. Popular items repeat. `positive_ids`: counted together with history_ids as stated there.
All inputs are finite; a program needn't handle non-finite values.
Results may differ from a plain program's by a relative error of at most 0.00012.
Values sent between devices are 32-bit elements; how exact they have to be, the bound alone decides.
A program may use at most 128 MiB of HBM per device.

v0:
```python
import jax
import jax.numpy as jnp
from jax import lax
from jax.sharding import PartitionSpec as P

penalty_weight = 10.0
step_size = 0.05


def owner_ranks(owner_dev, devices):
    total = owner_dev.shape[0]
    block = min(512, (total + 7) // 8 * 8)
    padded = (total + block - 1) // block * block
    owners_pad = jnp.concatenate([owner_dev, jnp.full((padded - total,), -1, jnp.int32)])
    owner_blocks = owners_pad.reshape(padded // block, block)
    lower = (
        jnp.arange(block, dtype=jnp.int32)[:, None] >= jnp.arange(block, dtype=jnp.int32)[None, :]
    ).astype(jnp.float32)
    columns = jnp.arange(devices, dtype=jnp.int32)[None, :]

    def step(carry, owners_blk):
        member = (owners_blk[:, None] == columns).astype(jnp.float32)
        prefix = jnp.dot(lower, member, preferred_element_type=jnp.float32)
        before = jnp.sum(member * carry[None, :], axis=1)
        ranks = jnp.sum(prefix * member, axis=1) + before - 1.0
        return (carry + jnp.sum(member, axis=0), ranks.astype(jnp.int32))

    start = jnp.zeros((devices,), jnp.float32)
    final, ranks = lax.scan(step, start, owner_blocks)
    return ranks.reshape(-1)[:total]


def shards(item_table, adagrad_state, history_ids, positive_ids):
    rows_dev, width = item_table.shape
    users_dev, hist_len = history_ids.shape
    n_data = lax.axis_size("dp")
    n_shard = lax.axis_size("rows")
    devices = n_data * n_shard
    requests = jnp.concatenate([history_ids, positive_ids[:, None]], axis=1).reshape(-1)
    request_count = requests.shape[0]
    capacity = max(8, (request_count * 5 // (2 * devices) + 7) // 8 * 8)
    owner_dev = requests // rows_dev
    local_row = requests % rows_dev
    slot_rank = owner_ranks(owner_dev, devices)
    flat_slot = owner_dev * capacity + slot_rank
    inverse = (
        jnp.full((devices * capacity,), request_count, jnp.int32)
        .at[flat_slot]
        .set(jnp.arange(request_count, dtype=jnp.int32))
    )
    local_pad = jnp.concatenate([local_row, jnp.full((1,), -1, jnp.int32)])
    wanted = jnp.take(local_pad, inverse, axis=0)
    item_gram = jnp.dot(
        item_table.T,
        item_table,
        precision=lax.Precision.HIGHEST,
        preferred_element_type=jnp.float32,
    )
    asked = lax.all_to_all(
        wanted.reshape(devices, capacity), ("dp", "rows"), split_axis=0, concat_axis=0, tiled=True
    )
    present = asked >= 0
    picked = jnp.take(item_table, jnp.where(present, asked, 0), axis=0)
    fetched_rows = lax.all_to_all(
        picked * present[..., None].astype(jnp.float32),
        ("dp", "rows"),
        split_axis=0,
        concat_axis=0,
        tiled=True,
    )
    request_rows = jnp.take(
        fetched_rows.reshape(devices * capacity, width), flat_slot, axis=0
    ).reshape(users_dev, hist_len + 1, width)
    user_vecs = jnp.sum(request_rows[:, :hist_len], axis=1) / hist_len
    positive_vecs = request_rows[:, hist_len]
    score_gap = jnp.sum(user_vecs * positive_vecs, axis=1) - 1.0
    user_gram = jnp.dot(
        user_vecs.T, user_vecs, precision=lax.Precision.HIGHEST, preferred_element_type=jnp.float32
    )
    user_total, item_total = lax.psum((user_gram, item_gram), ("dp", "rows"))
    penalty_coef = penalty_weight / (rows_dev * devices)
    user_grad = 2.0 * score_gap[:, None] * positive_vecs + 2.0 * penalty_coef * jnp.dot(
        user_vecs, item_total, precision=lax.Precision.HIGHEST, preferred_element_type=jnp.float32
    )
    positive_grad = 2.0 * score_gap[:, None] * user_vecs
    per_history = jnp.broadcast_to((user_grad / hist_len)[:, None, :], (users_dev, hist_len, width))
    request_grad = jnp.concatenate([per_history, positive_grad[:, None, :]], axis=1).reshape(
        -1, width
    )
    grad_pad = jnp.concatenate([request_grad, jnp.zeros((1, width), jnp.float32)], axis=0)
    outgoing = jnp.take(grad_pad, inverse, axis=0)
    returned = lax.all_to_all(
        outgoing.reshape(devices, capacity, width),
        ("dp", "rows"),
        split_axis=0,
        concat_axis=0,
        tiled=True,
    )
    present = asked >= 0
    target_rows = jnp.where(present, asked, 0).reshape(-1)
    masked_grad = (returned * present[..., None].astype(jnp.float32)).reshape(-1, width)
    row_grad = (
        2.0
        * penalty_coef
        * jnp.dot(
            item_table,
            user_total,
            precision=lax.Precision.HIGHEST,
            preferred_element_type=jnp.float32,
        )
    )
    row_grad = row_grad.at[target_rows].add(masked_grad)
    new_state = adagrad_state + row_grad * row_grad
    new_table = item_table - step_size * row_grad / jnp.sqrt(new_state)
    return (new_table, new_state)


def solution(mesh):
    return jax.shard_map(
        shards,
        mesh=mesh,
        in_specs=(
            P(("dp", "rows"), None),
            P(("dp", "rows"), None),
            P(("dp", "rows"), None),
            P(("dp", "rows")),
        ),
        out_specs=(P(("dp", "rows"), None), P(("dp", "rows"), None)),
        check_vma=False,
    )
```

profile of v0, /device:TPU:0, one launch (start us, length us, event | category | flops | bytes accessed | tf_op | source)
XLA Modules:
  0.0 951.0 jit_solution(10827428397425280180)
XLA Ops:
  7.2 0.8 pad_add_fusion
  8.1 0.2 reshape.200
  8.3 7.2 while.15
  8.4 0.1 fusion.44
  8.5 0.3 fusion.46
  8.9 0.1 fusion.44
  9.0 0.3 fusion.46
  9.6 0.3 fusion.46
  10.1 0.3 fusion.46
  10.7 0.3 fusion.46
  11.2 0.3 fusion.46
  11.8 0.3 fusion.46
  12.3 0.3 fusion.46
  12.9 0.3 fusion.46
  13.4 0.3 fusion.46
  14.0 0.3 fusion.46
  14.5 0.3 fusion.46
  15.1 0.3 fusion.46
  15.5 31.1 %scatter_custom_fusion = s32[16384]{0:T(1024)S(1)} fusion(s32[6528]{0:T(1024)S(1)} %get-tuple-element.118, s32[6528]{0:T(1024)S(1)} %iota.16, s32[]{:T(128)} %constant.135.clone.1), kind=kCustom, calls=%fused_computation.67 | custom fusion | bytes 65540 | tf_op jit(solution)/shard_map/scatter | solution.py:49
  46.7 90.5 %gather_fusion = s32[16384]{0:T(1024)S(1)} fusion(s32[6529]{0:T(1024)S(1)} %pad_add_fusion.1, s32[16384]{0:T(1024)S(1)} %fusion.18), kind=kCustom, calls=%fused_computation | custom fusion | bytes 196608 | tf_op jit(solution)/shard_map/jit(_take)/gather | solution.py:52
  137.3 14.4 %all_to_all.25 = s32[32,1,512]{2,1,0:T(1,128)S(1)} all-to-all(s32[32,1,512]{2,1,0:T(1,128)S(1)} %bitcast.52), channel_id=1, replica_groups=mesh['dp'=4,'rows'=8] {'dp','rows'}, dimensions={0} | all-to-all | bytes 131072 | tf_op jit(solution)/shard_map/all_to_all | solution.py:59
  151.9 54.4 %gather_fusion.1 = f32[16384,128]{1,0:T(8,128)} fusion(f32[4096,128]{1,0:T(8,128)S(1)} %copy-done, s32[16384]{0:T(1024)S(1)} %broadcast_clamp_fusion), kind=kCustom, calls=%fused_computation.1 | custom fusion | bytes 16842752 | tf_op jit(solution)/shard_map/jit(_take)/gather | solution.py:63
  206.3 7.7 select_multiply_fusion
  214.1 3.8 all-to-all-start.1
  217.9 0.2 slice.12
  218.4 4.1 fusion.32
  222.5 185.1 %all-to-all-done.1 = f32[32,512,128]{2,1,0:T(8,128)} async-done(((f32[32,512,128]{2,1,0:T(8,128)}), f32[32,512,128]{2,1,0:T(8,128)}, u32[]{:S(2)}, u32[]{:S(2)}) %all-to-all-start.1) | async-done | bytes 8388640 | tf_op jit(solution)/shard_map/all_to_all | solution.py:64
  407.5 16.3 %gather_fusion.2 = f32[6528,128]{1,0:T(8,128)} fusion(f32[16384,128]{1,0:T(8,128)} %bitcast.5, s32[7168]{0:T(1024)S(1)} %pad_clamp_fusion), kind=kCustom, calls=%fused_computation.2 | custom fusion | bytes 6710784 | tf_op jit(solution)/shard_map/jit(_take)/gather | solution.py:71
  423.8 4.6 gather.23
  428.4 3.6 copy_select_fusion
  432.0 0.2 slice_reduce_fusion
  432.1 1.5 copy-done.1
  433.8 0.9 fusion.16
  434.8 121.3 %all-reduce.5.cloned.1.call-done = (f32[128,128]{1,0:T(8,128)}, f32[128,128]{1,0:T(8,128)}) async-done(((f32[128,128]{1,0:T(8,128)}, f32[128,128]{1,0:T(8,128)}), (f32[128,128]{1,0:T(8,128)}, f32[128,128]{1,0:T(8,128)})) %all-reduce.5.cloned.1.call-update) | async-done | bytes 131088 | tf_op jit(solution)/shard_map/psum | solution.py:80
  556.1 1.1 fusion.14
  557.2 0.2 broadcast_in_dim.90
  557.4 2.1 pad_maximum_fusion
  559.6 4.6 reshape.204
  564.1 4.0 concatenate.19
  568.1 56.4 %gather_fusion.3 = f32[16384,128]{1,0:T(8,128)} fusion(f32[6529,128]{1,0:T(8,128)} %concatenate.19, s32[16384]{0:T(1024)S(1)} %fusion.18), kind=kCustom, calls=%fused_computation.3 | custom fusion | bytes 16842752 | tf_op jit(solution)/shard_map/jit(_take)/gather | solution.py:91
  624.4 9.9 %broadcast_select_fusion.1 = f32[32,512,128]{2,1,0:T(8,128)} fusion(f32[32,512,128]{2,1,0:T(8,128)} %bitcast.48, pred[32,512]{1,0:T(8,128)(4,1)S(1)} %broadcast_in_dim.88), kind=kLoop, calls=%fused_computation.26 | loop fusion | flops 2097152 | bytes 16793600 | tf_op jit(solution)/shard_map/jit(_take)/select_n | solution.py:91
  634.4 4.0 all-to-all-start.2
  638.5 3.3 fusion.12
  641.7 2.9 copy.27
  644.6 183.4 %all-to-all-done.2 = f32[32,512,128]{2,1,0:T(8,128)} async-done(((f32[32,512,128]{2,1,0:T(8,128)}), f32[32,512,128]{2,1,0:T(8,128)}, u32[]{:S(2)}, u32[]{:S(2)}) %all-to-all-start.2) | async-done | bytes 8388640 | tf_op jit(solution)/shard_map/all_to_all | solution.py:92
  828.0 7.9 broadcast_multiply_fusion
  835.9 103.6 %scatter_fusion = f32[4096,128]{1,0:T(8,128)} fusion(f32[4096,128]{1,0:T(8,128)} %copy.27, s32[16384]{0:T(1024)S(1)} %bitcast.51, f32[16384,128]{1,0:T(8,128)} %bitcast.46), kind=kCustom, calls=%fused_computation.5 | custom fusion | flops 2097152 | bytes 25231360 | tf_op jit(solution)/shard_map/scatter-add | solution.py:112
  939.5 4.6 multiply_subtract_fusion
  (110 shorter events, 3.5 us)
Async XLA Ops:
  46.7 105.1 %copy-start = (f32[4096,128]{1,0:T(8,128)S(1)}, f32[4096,128]{1,0:T(8,128)}, u32[]{:S(2)}) copy-start(f32[4096,128]{1,0:T(8,128)} %param.6) | copy-start | bytes 6291460
  214.1 4.2 copy-start.2
  214.1 4.3 copy-start.4
  214.1 193.5 %all-to-all-start.1 = ((f32[32,512,128]{2,1,0:T(8,128)}), f32[32,512,128]{2,1,0:T(8,128)}, u32[]{:S(2)}, u32[]{:S(2)}) async-start(f32[32,512,128]{2,1,0:T(8,128)} %select_multiply_fusion), calls=%async_computation.1 | async-start | bytes 16777216 | tf_op jit(solution)/shard_map/all_to_all | solution.py:64
  217.9 338.2 %all-reduce.5.cloned.1.call-start = ((), (), s32[]{:S(2)}) async-start(), calls=%async_computation.3 | async-start | bytes 262144 | tf_op jit(solution)/shard_map/psum | solution.py:80
  432.0 1.7 copy-start.1
  634.4 4.1 copy-start.3
  634.4 193.6 %all-to-all-start.2 = ((f32[32,512,128]{2,1,0:T(8,128)}), f32[32,512,128]{2,1,0:T(8,128)}, u32[]{:S(2)}, u32[]{:S(2)}) async-start(f32[32,512,128]{2,1,0:T(8,128)} %broadcast_select_fusion.1), calls=%async_computation.2 | async-start | bytes 16777216 | tf_op jit(solution)/shard_map/all_to_all | solution.py:92
Sparse Core Ops, SparseCore 0:
  434.8 121.2 all-reduce.4
where the time goes:
time: 955 us; the launch traced here: 951 us
  waiting for transfers between devices  490 us (51%)
  local copies, waits for them, and re-layouts  268 us (28%)
  other arithmetic  143 us (15%)
  blocking collectives  14.4 us (2%)
  between operations  14.3 us (1%)
  matrix products  12.9 us (1%)
    all_to_all x1, waiting for transfers between devices, shards(): lax.all_to_all(picked * present[..., None].astype(jnp.float32), ('dp', 'r...  185 us
    all_to_all x1, waiting for transfers between devices, shards(): lax.all_to_all(outgoing.reshape(devices, capacity, width), ('dp', 'rows')...  183 us
    psum x1, waiting for transfers between devices, shards(): user_total, item_total = lax.psum((user_gram, item_gram), ('dp', 'rows'))  121 us
    scatter-add x1, other arithmetic, shards(): row_grad = row_grad.at[target_rows].add(masked_grad)  104 us
    gather x1, local copies, waits for them, and re-layouts, shards(): wanted = jnp.take(local_pad, inverse, axis=0)  90.5 us
    gather x1, local copies, waits for them, and re-layouts, shards(): outgoing = jnp.take(grad_pad, inverse, axis=0)  56.4 us
    gather x1, local copies, waits for them, and re-layouts, shards(): picked = jnp.take(item_table, jnp.where(present, asked, 0), axis=0)  54.4 us
    scatter x1, local copies, waits for them, and re-layouts, shards(): inverse = jnp.full((devices * capacity,), request_count, jnp.int32).at[fl...  31.1 us
  transfers between devices with their start and end apart: 3, of which 3 were waited for; matrix products, arithmetic and copies ran while one was open for 1% of the time, Pallas kernels for 0%

commit v1 on v0

v1 whole, which is shorter than its diff:
```python
import functools

import jax
import jax.numpy as jnp
from jax import lax
from jax.experimental import pallas as pl
from jax.experimental.pallas import tpu as pltpu
from jax.sharding import PartitionSpec as P

penalty_weight = 10.0
step_size = 0.05
LOW = 128
STREAMS = 8
HIGHEST = lax.Precision.HIGHEST
f32, bf16, i32 = jnp.float32, jnp.bfloat16, jnp.int32


def round_up(value, unit):
    return (value + unit - 1) // unit * unit


def route_kernel(devices, capacity, users_dev, block, owner_ref, local_ref, code_ref, out_ref, acc):
    blocks = owner_ref.shape[1] // block
    upper = (
        lax.broadcasted_iota(i32, (block, block), 0) <= lax.broadcasted_iota(i32, (block, block), 1)
    ).astype(bf16)
    owners = lax.broadcasted_iota(i32, (devices, block), 0)
    ranks_to = lax.broadcasted_iota(i32, (capacity, block), 0)
    acc[...] = jnp.zeros_like(acc)
    carry = jnp.zeros((devices, 1), f32)
    for j in range(blocks):
        cols = slice(j * block, (j + 1) * block)
        local = local_ref[:, cols]
        high = (local // LOW).astype(f32)
        low = (local % LOW).astype(f32)
        code = code_ref[:, cols].astype(f32)
        member = (owner_ref[:, cols] == owners).astype(f32)
        prefix = jnp.dot(member.astype(bf16), upper, preferred_element_type=f32)
        rank = jnp.sum(member * (prefix + carry), axis=0, keepdims=True) - 1.0
        carry = carry + jnp.sum(member, axis=1, keepdims=True)
        left = jnp.concatenate(
            [member * high, member * low, member * code, member], axis=0
        ).astype(bf16)
        right = (rank.astype(i32) == ranks_to).astype(f32).astype(bf16)
        acc[...] += lax.dot_general(
            left, right, (((1,), (1,)), ((), ())), preferred_element_type=f32
        )
    row = acc[0:devices] * LOW + acc[devices : 2 * devices]
    code = acc[2 * devices : 3 * devices]
    present = acc[3 * devices : 4 * devices]
    empty = 2 * users_dev
    out_ref[0] = row.astype(i32)
    out_ref[1] = jnp.where(present > 0.5, code, float(empty)).astype(i32)


def split2(x):
    hi = x.astype(bf16)
    return hi, (x - hi.astype(f32)).astype(bf16)


def partial_kernel(devices, capacity, groups, unroll, rows_ref, code_ref, table_ref, out_ref, picked):
    width = table_ref.shape[1]
    codes_to = lax.broadcasted_iota(i32, (groups, capacity), 0)

    def one(b, _):
        base = b * capacity

        def gather(s, _):
            for k in range(unroll):
                e = s * unroll + k
                r = rows_ref[base + e]
                picked[pl.ds(e, 1), :] = table_ref[pl.ds(r, 1), :]
            return 0

        lax.fori_loop(0, capacity // unroll, gather, 0)
        x = picked[...]
        a0, a1 = split2(x)
        a2 = (x - a0.astype(f32) - a1.astype(f32)).astype(bf16)
        hot = (code_ref[b] == codes_to).astype(f32).astype(bf16)
        both = jnp.dot(hot, jnp.concatenate([a0, a1], axis=1), preferred_element_type=f32)
        last = jnp.dot(hot, a2, preferred_element_type=f32)
        out_ref[pl.ds(pl.multiple_of(b * groups, 8), groups), :] = both[:, :width] + (both[:, width:] + last)
        return 0

    lax.fori_loop(0, devices, one, 0)


def update_kernel(
    devices, users_dev, hist_len, coef, entries, unroll,
    rows_ref, gidx_ref, sums_ref, gram_ref, table_ref, state_ref, new_table_ref, new_state_ref,
    grads, ugram, *accs,
):
    groups = 2 * users_dev
    total = devices * groups
    item_total = gram_ref[...]
    ugram[...] = jnp.zeros_like(ugram)
    grads[pl.ds(total, 8), :] = jnp.zeros((8, grads.shape[1]), f32)

    def user(b, _):
        at = pl.multiple_of(b * groups, 8)
        at2 = pl.multiple_of(b * groups + users_dev, 8)
        uv = sums_ref[pl.ds(at, users_dev), :] / hist_len
        pv = sums_ref[pl.ds(at2, users_dev), :]
        gap = jnp.sum(uv * pv, axis=1, keepdims=True) - 1.0
        ug = 2.0 * gap * pv + 2.0 * coef * jnp.dot(
            uv, item_total, precision=HIGHEST, preferred_element_type=f32
        )
        grads[pl.ds(at, users_dev), :] = ug / hist_len
        grads[pl.ds(at2, users_dev), :] = 2.0 * gap * uv
        ugram[...] += lax.dot_general(
            uv, uv, (((0,), (0,)), ((), ())), precision=HIGHEST, preferred_element_type=f32
        )
        return 0

    lax.fori_loop(0, devices, user, 0)
    for acc in accs:
        acc[...] = jnp.zeros_like(acc)
    part = entries // len(accs)

    def scatter(s, _):
        for q in range(unroll):
            rows = [rows_ref[k * part + s * unroll + q] for k in range(len(accs))]
            gidx = [gidx_ref[k * part + s * unroll + q] for k in range(len(accs))]
            vals = [
                acc[pl.ds(r, 1), :] + grads[pl.ds(g, 1), :] for acc, r, g in zip(accs, rows, gidx)
            ]
            for acc, r, v in zip(accs, rows, vals):
                acc[pl.ds(r, 1), :] = v
        return 0

    lax.fori_loop(0, part // unroll, scatter, 0)
    tile = 256
    rows_dev = table_ref.shape[0]
    user_total = ugram[...]

    def finish(t, _):
        at = pl.ds(pl.multiple_of(t * tile, 8), tile)
        item = table_ref[at, :]
        g = 2.0 * coef * jnp.dot(item, user_total, precision=HIGHEST, preferred_element_type=f32)
        add = accs[0][at, :]
        for acc in accs[1:]:
            add = add + acc[at, :]
        g = g + add
        state = state_ref[at, :] + g * g
        new_state_ref[at, :] = state
        new_table_ref[at, :] = item - step_size * g / jnp.sqrt(state)
        return 0

    lax.fori_loop(0, rows_dev // tile, finish, 0)


VM = pl.BlockSpec(memory_space=pltpu.VMEM)
SM = pl.BlockSpec(memory_space=pltpu.SMEM)
PARAMS = pltpu.CompilerParams(vmem_limit_bytes=60 * 1024 * 1024)


def shards(item_table, adagrad_state, history_ids, positive_ids):
    rows_dev, width = item_table.shape
    users_dev, hist_len = history_ids.shape
    devices = lax.axis_size("dp") * lax.axis_size("rows")
    groups = 2 * users_dev
    count = users_dev * (hist_len + 1)
    capacity = max(8, (count * 5 // (2 * devices) + 7) // 8 * 8)
    block = 512
    padded = round_up(count, block)
    requests = jnp.concatenate([history_ids.reshape(-1), positive_ids])
    code = jnp.concatenate(
        [jnp.arange(users_dev * hist_len, dtype=i32) // hist_len, users_dev + jnp.arange(users_dev, dtype=i32)]
    )
    requests = jnp.pad(requests, (0, padded - count), constant_values=devices * rows_dev)
    code = jnp.pad(code, (0, padded - count))
    owner = requests // rows_dev
    local = requests - owner * rows_dev

    lists = pl.pallas_call(
        functools.partial(route_kernel, devices, capacity, users_dev, block),
        out_shape=jax.ShapeDtypeStruct((2, devices, capacity), i32),
        in_specs=[VM] * 3,
        out_specs=VM,
        scratch_shapes=[pltpu.VMEM((4 * devices, capacity), f32)],
        compiler_params=PARAMS,
        name="route",
    )(owner[None], local[None], code[None])
    asked = lax.all_to_all(lists, ("dp", "rows"), split_axis=1, concat_axis=1, tiled=True)
    rows = asked[0].reshape(-1)
    codes = asked[1]
    entries = devices * capacity
    partial = pl.pallas_call(
        functools.partial(partial_kernel, devices, capacity, groups, 16),
        out_shape=jax.ShapeDtypeStruct((devices * groups, width), f32),
        in_specs=[SM, VM, VM],
        out_specs=VM,
        scratch_shapes=[pltpu.VMEM((capacity, width), f32)],
        compiler_params=PARAMS,
        name="partial",
    )(rows, codes[:, None, :], item_table)
    item_gram = jnp.dot(item_table.T, item_table, precision=HIGHEST, preferred_element_type=f32)
    sums, item_total = lax.psum((partial, item_gram), ("dp", "rows"))
    coef = penalty_weight / (rows_dev * devices)
    gidx = jnp.where(
        codes < groups, codes + groups * jnp.arange(devices, dtype=i32)[:, None], devices * groups
    ).reshape(-1)
    return pl.pallas_call(
        functools.partial(update_kernel, devices, users_dev, hist_len, coef, entries, 2),
        out_shape=(
            jax.ShapeDtypeStruct(item_table.shape, f32),
            jax.ShapeDtypeStruct(item_table.shape, f32),
        ),
        in_specs=[SM, SM, VM, VM, VM, VM],
        out_specs=(VM, VM),
        scratch_shapes=[
            pltpu.VMEM((devices * groups + 8, width), f32),
            pltpu.VMEM((width, width), f32),
        ]
        + [pltpu.VMEM((rows_dev, width), f32)] * STREAMS,
        compiler_params=PARAMS,
        name="update",
    )(rows, gidx, sums, item_total, item_table, adagrad_state)


def solution(mesh):
    return jax.shard_map(
        shards,
        mesh=mesh,
        in_specs=(
            P(("dp", "rows"), None),
            P(("dp", "rows"), None),
            P(("dp", "rows"), None),
            P(("dp", "rows")),
        ),
        out_specs=(P(("dp", "rows"), None), P(("dp", "rows"), None)),
        check_vma=False,
    )
```

time: 955 us -> 268 us (0.28)
  the two profiles are of different devices: /device:TPU:0 before, /device:TPU:29 now
where the time goes in v1:
time: 268 us; the launch traced here: 263 us
  waiting for transfers between devices  140 us (52%)
  Pallas kernels  89.1 us (33%)
  between operations  14.1 us (5%)
  matrix products  6.29 us (2%)
  starting transfers between devices  6.18 us (2%)
  local copies, waits for them, and re-layouts  5.38 us (2%)
    psum x1, waiting for transfers between devices, shards(): sums, item_total = lax.psum((partial, item_gram), ('dp', 'rows'))  140 us
    pallas_call x1, Pallas kernels, shards(): pl.pallas_call(functools.partial(update_kernel, devices, users_dev, hist_...  47.9 us
    pallas_call x1, Pallas kernels, shards(): pl.pallas_call(functools.partial(partial_kernel, devices, capacity, group...  35.1 us
    dot_general x1, matrix products, shards(): jnp.dot(item_table.T, item_table, precision=HIGHEST, preferred_element_ty...  6.29 us
    all_to_all x1, starting transfers between devices, shards(): lax.all_to_all(lists, ('dp', 'rows'), split_axis=1, concat_axis=1, tiled=...  6.13 us
    pallas_call x1, Pallas kernels, shards(): pl.pallas_call(functools.partial(route_kernel, devices, capacity, users_d...  6.13 us
  transfers between devices with their start and end apart: 2, of which 1 were waited for; matrix products, arithmetic and copies ran while one was open for 3% of the time, Pallas kernels for 0%

profile of v1, /device:TPU:29, one launch (start us, length us, event | category | flops | bytes accessed | tf_op | source)
XLA Modules:
  0.0 262.7 jit_solution(4086734656034743925)
XLA Ops:
  7.2 0.6 broadcast_in_dim.16.code_ref
  7.8 0.8 copy.7
  8.7 0.1 reshape.15
  8.8 0.7 pad_add_fusion
  9.5 0.6 broadcast_in_dim.15.local_ref
  10.2 0.6 broadcast_in_dim.14.owner_ref
  10.8 6.1 %route.1 = s32[2,32,512]{2,1,0:T(8,128)} custom-call(s32[1,6656]{1,0:T(1,128)} %broadcast_in_dim.14.owner_ref, s32[1,6656]{1,0:T(1,128)} %broadcast_in_dim.15.local_ref, s32[1,6656]{1,0:T(1,128)} %broadcast_in_dim.16.code_ref), custom_call_target="tpu_custom_call" | custom-call | tf_op jit(solution)/shard_map/route/pallas_call | solution.py:175
  16.9 1.7 copy.8
  18.6 6.1 %all-to-all-start = ((s32[2,32,512]{2,0,1:T(2,128)}), s32[2,32,512]{2,0,1:T(2,128)S(1)}, u32[]{:S(2)}, u32[]{:S(2)}) async-start(s32[2,32,512]{2,0,1:T(2,128)} %copy.8), calls=%async_computation | async-start | bytes 262144 | tf_op jit(solution)/shard_map/all_to_all | solution.py:184
  24.7 0.0 all-reduce.5.cloned.1.call-start
  24.8 6.3 %fusion.5 = f32[128,128]{1,0:T(8,128)} fusion(f32[4096,128]{1,0:T(8,128)} %table_ref.3), kind=kOutput, calls=%fused_computation.22 | convolution fusion | flops 805306368 | bytes 2162688 | tf_op jit(solution)/shard_map/dot_general | solution.py:197
  31.1 0.0 all-to-all-done
  31.1 0.8 slice_bitcast_fusion
  31.8 35.1 %partial.1 = f32[8192,128]{1,0:T(8,128)} custom-call(s32[16384]{0:T(1024)} %bitcast.9, s32[32,1,512]{2,1,0:T(1,128)} %get-tuple-element.4.code_ref, f32[4096,128]{1,0:T(8,128)} %table_ref.3), custom_call_target="tpu_custom_call" | custom-call | tf_op jit(solution)/shard_map/partial/pallas_call | solution.py:188
  66.9 0.0 all-reduce.5.cloned.1.call-update
  66.9 0.1 broadcast_bitcast_fusion
  67.0 0.6 add_select_fusion.gidx_ref
  67.7 140.3 %all-reduce.5.cloned.1.call-done = (f32[8192,128]{1,0:T(8,128)}, f32[128,128]{1,0:T(8,128)}) async-done(((f32[8192,128]{1,0:T(8,128)}, f32[128,128]{1,0:T(8,128)}), (f32[8192,128]{1,0:T(8,128)}, f32[128,128]{1,0:T(8,128)})) %all-reduce.5.cloned.1.call-update) | async-done | bytes 4259856 | tf_op jit(solution)/shard_map/psum | solution.py:198
  207.9 47.9 %update.1 = (f32[4096,128]{1,0:T(8,128)}, f32[4096,128]{1,0:T(8,128)}) custom-call(s32[16384]{0:T(1024)} %bitcast.10, s32[16384]{0:T(1024)} %add_select_fusion.gidx_ref, f32[8192,128]{1,0:T(8,128)} %get-tuple-element.2.sums_ref, f32[128,128]{1,0:T(8,128)} %get-tuple-element.3.gram_ref, f32[4096,128]{1,0:T(8,128)} %table_ref.3, f32[4096,128]{1,0:T(8,128)} %state_ref.1), custom_call_target="tpu_custom_call" | custom-call | tf_op jit(solution)/shard_map/update/pallas_call | solution.py:203
  (7 shorter events, 0.1 us)
Async XLA Ops:
  18.6 12.5 %all-to-all-start = ((s32[2,32,512]{2,0,1:T(2,128)}), s32[2,32,512]{2,0,1:T(2,128)S(1)}, u32[]{:S(2)}, u32[]{:S(2)}) async-start(s32[2,32,512]{2,0,1:T(2,128)} %copy.8), calls=%async_computation | async-start | bytes 262144 | tf_op jit(solution)/shard_map/all_to_all | solution.py:184
  24.7 183.2 %all-reduce.5.cloned.1.call-start = ((), (), s32[]{:S(2)}) async-start(), calls=%async_computation.1 | async-start | bytes 8519680 | tf_op jit(solution)/shard_map/psum | solution.py:198
Sparse Core Ops, SparseCore 0:
  67.0 140.8 all-reduce.4

commit v2 on v1

--- a/solution.py
+++ b/solution.py
@@ -58,7 +58,7 @@
     return hi, (x - hi.astype(f32)).astype(bf16)
 
 
-def partial_kernel(devices, capacity, groups, unroll, rows_ref, code_ref, table_ref, out_ref, picked):
+def partial_kernel(devices, capacity, groups, unroll, rows_ref, code_ref, gram_ref, table_ref, out_ref, picked):
     width = table_ref.shape[1]
     codes_to = lax.broadcasted_iota(i32, (groups, capacity), 0)
 
@@ -79,28 +79,127 @@
         hot = (code_ref[b] == codes_to).astype(f32).astype(bf16)
         both = jnp.dot(hot, jnp.concatenate([a0, a1], axis=1), preferred_element_type=f32)
         last = jnp.dot(hot, a2, preferred_element_type=f32)
-        out_ref[pl.ds(pl.multiple_of(b * groups, 8), groups), :] = both[:, :width] + (both[:, width:] + last)
+        out_ref[b, 0:groups, :] = both[:, :width] + (both[:, width:] + last)
+        out_ref[b, groups:, :] = gram_ref[b]
         return 0
 
     lax.fori_loop(0, devices, one, 0)
+
+
+def reduce_kernel(data, shard, part_ref, out_ref, held, got, send1, recv1, send2, recv2, send3, recv3, send4, recv4):
+    peers = data // 2 * shard
+    dp, rw = lax.axis_index("dp"), lax.axis_index("rows")
+    core = lax.rem(dp, 2)
+    flat = dp // 2 * shard + rw
+    other = (dp + 1 - 2 * core, rw)
+    mesh_id = pl.DeviceIdType.MESH
+
+    def place(k):
+        at = lax.rem(flat + k, peers)
+        return at // shard * 2 + core, lax.rem(at, shard)
+
+    def slab(k, side):
+        d, r = place(k)
+        return (d + (1 - 2 * core) * side) * shard + r
+
+    barrier = pltpu.get_barrier_semaphore()
+    pl.semaphore_signal(barrier, inc=1, device_id=other, device_id_type=mesh_id)
+
+    def greet(k, _):
+        pl.semaphore_signal(barrier, inc=1, device_id=place(k), device_id_type=mesh_id)
+        return 0
+
+    lax.fori_loop(1, peers, greet, 0)
+    pl.semaphore_wait(barrier, peers)
+
+    def remote(src, dst, send, recv, device):
+        return pltpu.make_async_remote_copy(
+            src_ref=src, dst_ref=dst, send_sem=send, recv_sem=recv, device_id=device, device_id_type=mesh_id
+        )
+
+    def copy1(k):
+        return remote(part_ref.at[slab(k, 1)], held.at[k], send1.at[k], recv1.at[k], other)
+
+    def copy2(k):
+        return remote(held.at[k], got.at[k], send2.at[k], recv2.at[k], place(k))
+
+    def copy3(k):
+        mine = out_ref.at[slab(0, 0)]
+        return remote(mine, mine, send3.at[k], recv3.at[k], place(k))
+
+    def copy4(k):
+        at = out_ref.at[slab(peers - k, 0)]
+        return remote(at, at, send4.at[k], recv4.at[k], other)
+
+    def each(first, count, act):
+        def step(k, _):
+            act(k)
+            return 0
+
+        lax.fori_loop(first, count, step, 0)
+
+    def start1(k):
+        copy1(lax.rem(k, peers)).start()
+
+    each(1, peers + 1, start1)
+
+    def pair(k):
+        copy1(k).wait_recv()
+        held[k] = held[k] + part_ref[slab(k, 0)]
+        copy2(k).start()
+
+    each(1, peers, pair)
+    copy1(0).wait_recv()
+    held[0] = held[0] + part_ref[slab(0, 0)]
+
+    def gain(k):
+        copy2(k).wait_recv()
+        held[0] = held[0] + got[k]
+
+    each(1, peers, gain)
+    out_ref[slab(0, 0)] = held[0]
+    each(1, peers, lambda k: copy3(k).start())
+    copy4(0).start()
+
+    def forward(k):
+        copy3(k).wait_recv()
+        copy4(k).start()
+
+    each(1, peers, forward)
+    each(0, peers, lambda k: copy4(k).wait_recv())
+
+    def drain(k):
+        copy1(k).wait_send()
+        copy4(k).wait_send()
+
+    each(0, peers, drain)
+
+    def drain2(k):
+        copy2(k).wait_send()
+        copy3(k).wait_send()
+
+    each(1, peers, drain2)
 
 
 def update_kernel(
     devices, users_dev, hist_len, coef, entries, unroll,
-    rows_ref, gidx_ref, sums_ref, gram_ref, table_ref, state_ref, new_table_ref, new_state_ref,
+    rows_ref, gidx_ref, sums_ref, table_ref, state_ref, new_table_ref, new_state_ref,
     grads, ugram, *accs,
 ):
     groups = 2 * users_dev
     total = devices * groups
-    item_total = gram_ref[...]
+    extra = sums_ref.shape[1] - groups
+    for t in range(ugram.shape[0] // extra):
+        ugram[t * extra : (t + 1) * extra, :] = sums_ref[t, groups:, :]
+    item_total = ugram[...]
     ugram[...] = jnp.zeros_like(ugram)
     grads[pl.ds(total, 8), :] = jnp.zeros((8, grads.shape[1]), f32)
 
     def user(b, _):
         at = pl.multiple_of(b * groups, 8)
         at2 = pl.multiple_of(b * groups + users_dev, 8)
-        uv = sums_ref[pl.ds(at, users_dev), :] / hist_len
-        pv = sums_ref[pl.ds(at2, users_dev), :]
+        uv = sums_ref[b, 0:users_dev, :] / hist_len
+        pv = sums_ref[b, users_dev:groups, :]
         gap = jnp.sum(uv * pv, axis=1, keepdims=True) - 1.0
         ug = 2.0 * gap * pv + 2.0 * coef * jnp.dot(
             uv, item_total, precision=HIGHEST, preferred_element_type=f32
@@ -185,17 +284,32 @@
     rows = asked[0].reshape(-1)
     codes = asked[1]
     entries = devices * capacity
+    item_gram = jnp.dot(item_table.T, item_table, precision=HIGHEST, preferred_element_type=f32)
+    extra = round_up(-(-width // devices), 8)
+    chunk = groups + extra
+    gram_rows = jnp.pad(item_gram, ((0, devices * extra - width), (0, 0))).reshape(devices, extra, width)
     partial = pl.pallas_call(
         functools.partial(partial_kernel, devices, capacity, groups, 16),
-        out_shape=jax.ShapeDtypeStruct((devices * groups, width), f32),
-        in_specs=[SM, VM, VM],
+        out_shape=jax.ShapeDtypeStruct((devices, chunk, width), f32),
+        in_specs=[SM, VM, VM, VM],
         out_specs=VM,
         scratch_shapes=[pltpu.VMEM((capacity, width), f32)],
         compiler_params=PARAMS,
         name="partial",
-    )(rows, codes[:, None, :], item_table)
-    item_gram = jnp.dot(item_table.T, item_table, precision=HIGHEST, preferred_element_type=f32)
-    sums, item_total = lax.psum((partial, item_gram), ("dp", "rows"))
+    )(rows, codes[:, None, :], gram_rows, item_table)
+    data, shard = lax.axis_size("dp"), lax.axis_size("rows")
+    peers = devices // 2
+    sums = pl.pallas_call(
+        functools.partial(reduce_kernel, data, shard),
+        out_shape=jax.ShapeDtypeStruct((devices, chunk, width), f32),
+        in_specs=[VM],
+        out_specs=VM,
+        scratch_shapes=[pltpu.VMEM((peers, chunk, width), f32)] * 2 + [pltpu.SemaphoreType.DMA((peers,))] * 8,
+        compiler_params=pltpu.CompilerParams(
+            vmem_limit_bytes=60 * 1024 * 1024, collective_id=0, has_side_effects=True
+        ),
+        name="reduce",
+    )(partial)
     coef = penalty_weight / (rows_dev * devices)
     gidx = jnp.where(
         codes < groups, codes + groups * jnp.arange(devices, dtype=i32)[:, None], devices * groups
@@ -206,7 +320,7 @@
             jax.ShapeDtypeStruct(item_table.shape, f32),
             jax.ShapeDtypeStruct(item_table.shape, f32),
         ),
-        in_specs=[SM, SM, VM, VM, VM, VM],
+        in_specs=[SM, SM, VM, VM, VM],
         out_specs=(VM, VM),
         scratch_shapes=[
             pltpu.VMEM((devices * groups + 8, width), f32),
@@ -215,7 +329,7 @@
         + [pltpu.VMEM((rows_dev, width), f32)] * STREAMS,
         compiler_params=PARAMS,
         name="update",
-    )(rows, gidx, sums, item_total, item_table, adagrad_state)
+    )(rows, gidx, sums, item_table, adagrad_state)
 
 
 def solution(mesh):

time: 268 us -> 221 us (0.82); the launches traced: 263 us -> 221 us
  waiting for transfers between devices: 140 us -> 0.01 us
  Pallas kernels: 89.1 us -> 201 us
  between operations: 14.1 us -> 0.7 us
    psum x1 -> x0, waiting for transfers between devices: 140 us -> none  [shards(): sums, item_total = lax.psum((partial, item_gram), ('dp', 'rows'))]
    pallas_call x0 -> x1, Pallas kernels: none -> 112 us  [shards(): pl.pallas_call(functools.partial(reduce_kernel, data, shard), out_shape=j...]
  transfers between devices with their start and end apart: 2 -> 1, of which waited for: 1 -> 0; matrix products, arithmetic and copies ran while one was open for 3% -> 3% of each run, Pallas kernels for 0% -> 0%
where the time goes in v2:
time: 221 us
  Pallas kernels  201 us (91%)
  starting transfers between devices  6.13 us (3%)
  local copies, waits for them, and re-layouts  6.04 us (3%)
  matrix products  5.67 us (3%)
    pallas_call x1, Pallas kernels, shards(): pl.pallas_call(functools.partial(reduce_kernel, data, shard), out_shape=j...  112 us
    pallas_call x1, Pallas kernels, shards(): pl.pallas_call(functools.partial(update_kernel, devices, users_dev, hist_...  47.9 us
    pallas_call x1, Pallas kernels, shards(): pl.pallas_call(functools.partial(partial_kernel, devices, capacity, group...  35.4 us
    pallas_call x1, Pallas kernels, shards(): pl.pallas_call(functools.partial(route_kernel, devices, capacity, users_d...  6.14 us
    all_to_all x1, starting transfers between devices, shards(): lax.all_to_all(lists, ('dp', 'rows'), split_axis=1, concat_axis=1, tiled=...  6.13 us
    dot_general x1, matrix products, shards(): jnp.dot(item_table.T, item_table, precision=HIGHEST, preferred_element_ty...  5.67 us
  transfers between devices with their start and end apart: 1, of which 0 were waited for; matrix products, arithmetic and copies ran while one was open for 3% of the time, Pallas kernels for 0%

profile of v2, /device:TPU:29, one launch (start us, length us, event | category | flops | bytes accessed | tf_op | source)
XLA Modules:
  0.0 221.0 jit_solution(14280379767052844193)
XLA Ops:
  0.7 0.6 broadcast_in_dim.16.code_ref
  1.3 0.8 copy.7
  2.2 0.1 reshape.18
  2.3 0.7 pad_add_fusion
  3.0 0.6 broadcast_in_dim.15.local_ref
  3.6 0.6 broadcast_in_dim.14.owner_ref
  4.2 6.1 %route.1 = s32[2,32,512]{2,1,0:T(8,128)} custom-call(s32[1,6656]{1,0:T(1,128)} %broadcast_in_dim.14.owner_ref, s32[1,6656]{1,0:T(1,128)} %broadcast_in_dim.15.local_ref, s32[1,6656]{1,0:T(1,128)} %broadcast_in_dim.16.code_ref), custom_call_target="tpu_custom_call" | custom-call | tf_op jit(solution)/shard_map/route/pallas_call | solution.py:274
  10.4 1.7 copy.8
  12.0 6.1 %all-to-all-start = ((s32[2,32,512]{2,0,1:T(2,128)}), s32[2,32,512]{2,0,1:T(2,128)S(1)}, u32[]{:S(2)}, u32[]{:S(2)}) async-start(s32[2,32,512]{2,0,1:T(2,128)} %copy.8), calls=%async_computation | async-start | bytes 262144 | tf_op jit(solution)/shard_map/all_to_all | solution.py:283
  18.2 5.7 %fusion.5 = f32[128,128]{1,0:T(8,128)S(1)} fusion(f32[4096,128]{1,0:T(8,128)} %table_ref.3), kind=kOutput, calls=%fused_computation.23 | convolution fusion | flops 805306368 | bytes 2162688 | tf_op jit(solution)/shard_map/dot_general | solution.py:287
  23.9 0.1 broadcast_bitcast_fusion
  24.0 0.7 pad_bitcast_fusion.gram_ref
  24.6 0.0 all-to-all-done
  24.6 0.8 slice_bitcast_fusion
  25.4 35.4 %partial.1.part_ref = f32[32,264,128]{2,1,0:T(8,128)} custom-call(s32[16384]{0:T(1024)} %bitcast.11, s32[32,1,512]{2,1,0:T(1,128)} %get-tuple-element.2.code_ref, f32[32,8,128]{2,1,0:T(8,128)} %pad_bitcast_fusion.gram_ref, f32[4096,128]{1,0:T(8,128)} %table_ref.3), custom_call_target="tpu_custom_call" | custom-call | tf_op jit(solution)/shard_map/partial/pallas_call | solution.py:291
  60.8 111.7 %reduce.1.sums_ref = f32[32,264,128]{2,1,0:T(8,128)} custom-call(f32[32,264,128]{2,1,0:T(8,128)} %partial.1.part_ref), custom_call_target="tpu_custom_call" | custom-call | tf_op jit(solution)/shard_map/reduce/pallas_call | solution.py:302
  172.5 0.6 add_select_fusion.gidx_ref
  173.1 47.9 %update.1 = (f32[4096,128]{1,0:T(8,128)}, f32[4096,128]{1,0:T(8,128)}) custom-call(s32[16384]{0:T(1024)} %bitcast.12, s32[16384]{0:T(1024)} %add_select_fusion.gidx_ref, f32[32,264,128]{2,1,0:T(8,128)} %reduce.1.sums_ref, f32[4096,128]{1,0:T(8,128)} %table_ref.3, f32[4096,128]{1,0:T(8,128)} %state_ref.1), custom_call_target="tpu_custom_call" | custom-call | tf_op jit(solution)/shard_map/update/pallas_call | solution.py:317
  (7 shorter events, 0.1 us)
Async XLA Ops:
  12.0 12.6 %all-to-all-start = ((s32[2,32,512]{2,0,1:T(2,128)}), s32[2,32,512]{2,0,1:T(2,128)S(1)}, u32[]{:S(2)}, u32[]{:S(2)}) async-start(s32[2,32,512]{2,0,1:T(2,128)} %copy.8), calls=%async_computation | async-start | bytes 262144 | tf_op jit(solution)/shard_map/all_to_all | solution.py:283

commit v3 on v2

--- a/solution.py
+++ b/solution.py
@@ -289,7 +289,7 @@
     chunk = groups + extra
     gram_rows = jnp.pad(item_gram, ((0, devices * extra - width), (0, 0))).reshape(devices, extra, width)
     partial = pl.pallas_call(
-        functools.partial(partial_kernel, devices, capacity, groups, 16),
+        functools.partial(partial_kernel, devices, capacity, groups, 32),
         out_shape=jax.ShapeDtypeStruct((devices, chunk, width), f32),
         in_specs=[SM, VM, VM, VM],
         out_specs=VM,
@@ -315,7 +315,7 @@
         codes < groups, codes + groups * jnp.arange(devices, dtype=i32)[:, None], devices * groups
     ).reshape(-1)
     return pl.pallas_call(
-        functools.partial(update_kernel, devices, users_dev, hist_len, coef, entries, 2),
+        functools.partial(update_kernel, devices, users_dev, hist_len, coef, entries, 4),
         out_shape=(
             jax.ShapeDtypeStruct(item_table.shape, f32),
             jax.ShapeDtypeStruct(item_table.shape, f32),

time: 221 us -> 217 us (0.982)
  Pallas kernels: 201 us -> 197 us
where the time goes in v3:
time: 217 us
  Pallas kernels  197 us (91%)
  starting transfers between devices  6.13 us (3%)
  local copies, waits for them, and re-layouts  6.04 us (3%)
  matrix products  5.67 us (3%)
    pallas_call x1, Pallas kernels, shards(): pl.pallas_call(functools.partial(reduce_kernel, data, shard), out_shape=j...  112 us
    pallas_call x1, Pallas kernels, shards(): pl.pallas_call(functools.partial(update_kernel, devices, users_dev, hist_...  46 us
    pallas_call x1, Pallas kernels, shards(): pl.pallas_call(functools.partial(partial_kernel, devices, capacity, group...  33.3 us
    pallas_call x1, Pallas kernels, shards(): pl.pallas_call(functools.partial(route_kernel, devices, capacity, users_d...  6.14 us
    all_to_all x1, starting transfers between devices, shards(): lax.all_to_all(lists, ('dp', 'rows'), split_axis=1, concat_axis=1, tiled=...  6.13 us
    dot_general x1, matrix products, shards(): jnp.dot(item_table.T, item_table, precision=HIGHEST, preferred_element_ty...  5.67 us
  transfers between devices with their start and end apart: 1, of which 0 were waited for; matrix products, arithmetic and copies ran while one was open for 3% of the time, Pallas kernels for 0%

profile of v3, /device:TPU:29, one launch (start us, length us, event | category | flops | bytes accessed | tf_op | source)
XLA Modules:
  0.0 217.0 jit_solution(5536981369876161290)
XLA Ops:
  0.7 0.6 broadcast_in_dim.16.code_ref
  1.3 0.8 copy.7
  2.2 0.1 reshape.18
  2.3 0.7 pad_add_fusion
  3.0 0.6 broadcast_in_dim.15.local_ref
  3.6 0.6 broadcast_in_dim.14.owner_ref
  4.2 6.1 %route.1 = s32[2,32,512]{2,1,0:T(8,128)} custom-call(s32[1,6656]{1,0:T(1,128)} %broadcast_in_dim.14.owner_ref, s32[1,6656]{1,0:T(1,128)} %broadcast_in_dim.15.local_ref, s32[1,6656]{1,0:T(1,128)} %broadcast_in_dim.16.code_ref), custom_call_target="tpu_custom_call" | custom-call | tf_op jit(solution)/shard_map/route/pallas_call | solution.py:274
  10.4 1.7 copy.8
  12.0 6.1 %all-to-all-start = ((s32[2,32,512]{2,0,1:T(2,128)}), s32[2,32,512]{2,0,1:T(2,128)S(1)}, u32[]{:S(2)}, u32[]{:S(2)}) async-start(s32[2,32,512]{2,0,1:T(2,128)} %copy.8), calls=%async_computation | async-start | bytes 262144 | tf_op jit(solution)/shard_map/all_to_all | solution.py:283
  18.2 5.7 %fusion.5 = f32[128,128]{1,0:T(8,128)S(1)} fusion(f32[4096,128]{1,0:T(8,128)} %table_ref.3), kind=kOutput, calls=%fused_computation.23 | convolution fusion | flops 805306368 | bytes 2162688 | tf_op jit(solution)/shard_map/dot_general | solution.py:287
  23.9 0.1 broadcast_bitcast_fusion
  24.0 0.7 pad_bitcast_fusion.gram_ref
  24.6 0.0 all-to-all-done
  24.6 0.8 slice_bitcast_fusion
  25.4 33.3 %partial.1.part_ref = f32[32,264,128]{2,1,0:T(8,128)} custom-call(s32[16384]{0:T(1024)} %bitcast.11, s32[32,1,512]{2,1,0:T(1,128)} %get-tuple-element.2.code_ref, f32[32,8,128]{2,1,0:T(8,128)} %pad_bitcast_fusion.gram_ref, f32[4096,128]{1,0:T(8,128)} %table_ref.3), custom_call_target="tpu_custom_call" | custom-call | tf_op jit(solution)/shard_map/partial/pallas_call | solution.py:291
  58.7 111.7 %reduce.1.sums_ref = f32[32,264,128]{2,1,0:T(8,128)} custom-call(f32[32,264,128]{2,1,0:T(8,128)} %partial.1.part_ref), custom_call_target="tpu_custom_call" | custom-call | tf_op jit(solution)/shard_map/reduce/pallas_call | solution.py:302
  170.3 0.6 add_select_fusion.gidx_ref
  171.0 46.0 %update.1 = (f32[4096,128]{1,0:T(8,128)}, f32[4096,128]{1,0:T(8,128)}) custom-call(s32[16384]{0:T(1024)} %bitcast.12, s32[16384]{0:T(1024)} %add_select_fusion.gidx_ref, f32[32,264,128]{2,1,0:T(8,128)} %reduce.1.sums_ref, f32[4096,128]{1,0:T(8,128)} %table_ref.3, f32[4096,128]{1,0:T(8,128)} %state_ref.1), custom_call_target="tpu_custom_call" | custom-call | tf_op jit(solution)/shard_map/update/pallas_call | solution.py:317
  (7 shorter events, 0.1 us)
Async XLA Ops:
  12.0 12.6 %all-to-all-start = ((s32[2,32,512]{2,0,1:T(2,128)}), s32[2,32,512]{2,0,1:T(2,128)S(1)}, u32[]{:S(2)}, u32[]{:S(2)}) async-start(s32[2,32,512]{2,0,1:T(2,128)} %copy.8), calls=%async_computation | async-start | bytes 262144 | tf_op jit(solution)/shard_map/all_to_all | solution.py:283
